TPU v7x, 32 devices: a whole 2x2x4 slice. The times are simulated.
32 devices in a mesh: blk: 8 (over z, y), pix: 4 (over x, core).
Axes of the slice: x: 2, y: 2, z: 4, core: 2. Of those that a mesh axis runs over, the one named last changes fastest.
Arguments:
- pixels: bfloat16 [32768, 224], P(('blk', 'pix')), may hold values from -6 to 6
- bundles: bfloat16 [16, 224, 64], P('blk'), may hold values from -0.375 to 0.375
- assign: int32 [32768, 1], P(('blk', 'pix')), may hold values from 0 to 15; in each aligned block of 1024 rows (0 to 1023, 1024 to 2047, ...) at most 128 rows name the same one
Outputs:
- abundances: float32 [32768, 64], P(('blk', 'pix'))
- residual_energy: float32 [8, 16], P('blk')
Inputs may be any that keep to these rules, and one draw needn't show every extreme that they name: `assign`: among the 1024 rows of one device no bundle is named more than 128 times; in every draw some device names some bundle exactly 128 times; every bundle is named somewhere.
All inputs are finite; a program needn't handle non-finite values. Where the computation divides by a largest or mean magnitude, that divisor is 1e-20 or more.
Results may differ from a plain program's by a relative error of at most 0.0003.
Values may be sent and summed in bfloat16 or wider, within the bound.
A program may use at most 64 MiB of HBM per device.

v0:
```python
import jax
import jax.numpy as jnp
from jax import lax
from jax.sharding import PartitionSpec as P

ITERS = 8
sum_weight = 0.015625


def make_slots(assign, count, cap):
    labels = assign[:, 0]
    onehot = (labels[:, None] == jnp.arange(count, dtype=jnp.int32)[None, :]).astype(jnp.int32)
    ranked = jnp.sum(jnp.cumsum(onehot, axis=0) * onehot, axis=1) - 1
    return labels * cap + ranked


def gram_of(spectra):
    gram = (
        jnp.einsum("nbm,nbk->nmk", spectra, spectra, preferred_element_type=jnp.float32)
        + sum_weight
    )
    step = 1.0 / jnp.max(jnp.sum(jnp.abs(gram), axis=2), axis=1)
    return (gram, step)


def solve(blocks, spectra, gram, step):
    target = (
        jnp.einsum("nsb,nbm->nsm", blocks, spectra, preferred_element_type=jnp.float32) + sum_weight
    )

    def sweep(index, state):
        grad = jnp.einsum("nsm,nmk->nsk", state, gram, precision=lax.Precision.HIGHEST)
        return jnp.maximum(state - step[:, None, None] * (grad - target), 0.0)

    state = lax.fori_loop(0, ITERS, sweep, jnp.zeros_like(target))
    fitted = jnp.einsum(
        "nsm,nbm->nsb", state, spectra.astype(jnp.float32), precision=lax.Precision.HIGHEST
    )
    misfit = blocks.astype(jnp.float32) - fitted
    return (state, jnp.sum(misfit * misfit, axis=-1))


def per_device(pixels, bundles, assign):
    rows, bands = pixels.shape
    width = bundles.shape[2]
    owned = bundles.shape[0]
    count = lax.axis_size("blk") * owned
    cap = 2 * rows // count
    slots = make_slots(assign, count, cap)
    flat = jnp.zeros((count * cap, bands), jnp.bfloat16).at[slots].set(pixels)
    buckets = flat.reshape(count, cap, bands)
    valid = jnp.zeros((count * cap,), jnp.float32).at[slots].set(1.0).reshape(count, cap)
    piece = lax.all_gather(bundles, "blk", axis=0, tiled=True)
    grams, steps = gram_of(piece)
    state, misfit = solve(buckets, piece, grams, steps)
    chosen = state.reshape(count * cap, width)[slots]
    scale = bands * rows * lax.axis_size("pix") / count
    energy = jnp.sum(misfit * valid / scale, axis=1)
    total = lax.psum(energy, "pix")
    return (chosen, total[None, :])


def solution(mesh):
    placed = (P(("blk", "pix"), None), P("blk", None, None), P(("blk", "pix"), None))
    return jax.shard_map(
        per_device,
        mesh=mesh,
        in_specs=placed,
        out_specs=(P(("blk", "pix"), None), P("blk", None)),
        check_vma=False,
    )
```

profile of v0, /device:TPU:0, one launch (start us, length us, event | category | flops | bytes accessed | tf_op | source)
XLA Modules:
  0.0 69.8 jit_solution(9833450703897635159)
XLA Ops:
  0.6 0.0 copy-start
  0.6 0.7 %fusion.11 = s32[16,8,128]{2,1,0:T(8,128)S(1)} fusion(s32[8,128]{1,0:T(8,128)} %bitcast.42), kind=kLoop, calls=%fused_computation.22 | loop fusion | flops 32768 | bytes 69632 | tf_op jit(solution)/shard_map/convert_element_type | solution.py:12
  1.4 4.5 %reduce-window.6 = s32[16,8,128]{2,1,0:T(8,128)S(1)} reduce-window(s32[16,8,128]{2,1,0:T(8,128)S(1)} %fusion.11, s32[]{:T(128)} %constant.5.clone.1), window={size=1x1x128 pad=0_0x0_0x127_0}, to_apply=%region_2.3 | reduce-window | flops 2080768 | bytes 131076 | tf_op jit(solution)/shard_map/reduce-window
  5.9 0.1 slice.10
  6.0 0.1 copy.25
  6.1 0.1 copy.26
  6.2 0.1 broadcast_add_fusion
  6.3 0.7 %fusion.10 = s32[1024]{0:T(1024)S(1)} fusion(s32[2,8,8,128]{3,2,1,0:T(8,128)S(1)} %bitcast.41, s32[1024]{0:T(1024)} %bitcast.43), kind=kLoop, calls=%fused_computation.19 | loop fusion | flops 48128 | bytes 73728 | tf_op jit(solution)/shard_map/reduce_sum | solution.py:13
  7.0 0.7 %compare_select_fusion = s32[1024,1]{0,1:T(1,128)S(1)} fusion(s32[1024,1]{0,1:T(1,128)S(1)} %bitcast.48, s32[1024,1]{0,1:T(1,128)} %param.7), kind=kLoop, calls=%fused_computation.24 | loop fusion | flops 5120 | bytes 12288 | tf_op jit(solution)/shard_map/select_n | solution.py:50
  7.7 4.3 %scatter_custom_fusion.1 = f32[2048]{0:T(1024)S(1)} fusion(s32[1024]{0:T(1024)S(1)} %bitcast.45, f32[1024]{0:T(1024)S(1)} %broadcast.53, f32[]{:T(128)} %constant.17.clone.1), kind=kCustom, calls=%fused_computation.28 | custom fusion | bytes 8196 | tf_op jit(solution)/shard_map/scatter | solution.py:52
  12.1 33.2 %all_gather.3 = bf16[16,224,64]{1,2,0:T(8,128)(2,1)S(1)} all-gather(bf16[2,224,64]{1,2,0:T(8,128)(2,1)} %param.6), channel_id=1, replica_groups=mesh['blk'=8,'pix'=4] {'blk'}, dimensions={0}, use_global_device_ids=true | all-gather | bytes 516096 | tf_op jit(solution)/shard_map/all_gather | solution.py:53
  45.3 0.0 copy-done
  45.3 0.2 copy.27
  45.5 5.3 %scatter_custom_fusion = bf16[2048,224]{1,0:T(8,128)(2,1)S(1)} fusion(s32[1024]{0:T(1024)S(1)} %bitcast.47, bf16[1024,224]{1,0:T(8,128)(2,1)S(1)} %copy.27, bf16[]{:T(256)} %constant.21.clone.1), kind=kCustom, calls=%fused_computation.14 | custom fusion | bytes 917506 | tf_op jit(solution)/shard_map/scatter | solution.py:50
  50.8 0.5 convolution_add_fusion
  51.3 0.6 copy.29
  51.9 0.3 abs_reduce_fusion
  52.2 0.1 reduce_max.9
  52.4 6.0 %while.11 = (s32[]{:T(128)}, f32[16,128,64]{1,2,0:T(8,128)S(1)}, f32[16]{0:T(128)S(1)}, f32[16,64,64]{1,2,0:T(8,128)S(1)}, f32[16,128,64]{1,2,0:T(8,128)S(1)}, /*index=5*/s32[]{:T(128)}, s32[]{:T(128)}) while((s32[]{:T(128)}, f32[16,128,64]{1,2,0:T(8,128)S(1)}, f32[16]{0:T(128)S(1)}, f32[16,64,64]{1,2,0:T(8,128)S(1)}, ...), condition=%wide.region_7.8_spmd.clone, body=%wide.region_6.7_spmd.clone.sunk | while | flops 101449728 | bytes 2883735 | solution.py:35
  52.4 0.7 fusion.28
  53.2 0.7 fusion.28
  53.9 0.7 fusion.28
  54.7 0.7 fusion.28
  55.4 0.7 fusion.28
  56.2 0.7 fusion.28
  56.9 0.7 fusion.28
  57.7 0.7 fusion.28
  58.4 1.1 %multiply_reduce_fusion = f32[16,128]{1,0:T(8,128)S(1)} fusion(bf16[16,128,224]{1,2,0:T(8,128)(2,1)S(1)} %copy.29, f32[16,128,64]{1,2,0:T(8,128)S(1)} %get-tuple-element.29, bf16[16,224,64]{1,2,0:T(8,128)(2,1)S(1)} %all_gather.3), kind=kOutput, calls=%fused_computation.11 | convolution fusion | flops 354154496 | bytes 1908736 | tf_op jit(solution)/shard_map/nsm,nbm->nsb/dot_general | solution.py:36
  59.5 0.1 fusion.13
  59.6 6.2 %psum.7 = f32[1,16]{1,0:T(1,128)} all-reduce(f32[1,16]{1,0:T(1,128)S(1)} %bitcast.49), channel_id=1, replica_groups=mesh['blk'=8,'pix'=4] {'pix'}, use_global_device_ids=true, to_apply=%region_11.12 | all-reduce | flops 16 | bytes 128 | tf_op jit(solution)/shard_map/psum | solution.py:59
  65.8 0.3 copy.30
  66.1 2.8 %gather_fusion = f32[1024,64]{1,0:T(8,128)S(1)} fusion(f32[2048,64]{1,0:T(8,128)S(1)} %bitcast.38, s32[1024]{0:T(1024)S(1)} %broadcast_clamp_fusion), kind=kCustom, calls=%fused_computation | custom fusion | bytes 528384 | tf_op jit(solution)/shard_map/gather | solution.py:56
  68.9 0.9 %copy.32 = f32[1024,64]{0,1:T(8,128)} copy(f32[1024,64]{1,0:T(8,128)S(1)} %gather_fusion) | data formatting | bytes 524288
  (15 shorter events, 0.3 us)
Async XLA Ops:
  0.6 44.7 %copy-start = (bf16[1024,224]{0,1:T(8,128)(2,1)S(1)}, bf16[1024,224]{0,1:T(8,128)(2,1)}, u32[]{:S(2)}) copy-start(bf16[1024,224]{0,1:T(8,128)(2,1)} %param.5) | copy-start | bytes 1376260
where the time goes:
time: 70.1 us; the launch traced here: 69.8 us
  blocking collectives  39.4 us (56%)
  local copies, waits for them, and re-layouts  15 us (21%)
  matrix products  7.35 us (10%)
  other arithmetic  7.02 us (10%)
  between operations  0.75 us (1%)
    all_gather x1, blocking collectives, per_device(): piece = lax.all_gather(bundles, 'blk', axis=0, tiled=True)  33.2 us
    psum x1, blocking collectives, per_device(): total = lax.psum(energy, 'pix')  6.17 us
    dot_general x8, matrix products, sweep(): jnp.einsum('nsm,nmk->nsk', state, gram, precision=lax.Precision.HIGHEST)  5.45 us
    scatter x1, local copies, waits for them, and re-layouts, per_device(): flat = jnp.zeros((count * cap, bands), jnp.bfloat16).at[slots].set(pixels)  5.28 us
    another operation x3, other arithmetic  4.61 us
    scatter x1, local copies, waits for them, and re-layouts, per_device(): jnp.zeros((count * cap,), jnp.float32).at[slots].set(1.0)  4.32 us
    gather x1, local copies, waits for them, and re-layouts, per_device(): chosen = state.reshape(count * cap, width)[slots]  2.81 us

commit v1 on v0

--- a/solution.py
+++ b/solution.py
@@ -56,7 +56,7 @@
     chosen = state.reshape(count * cap, width)[slots]
     scale = bands * rows * lax.axis_size("pix") / count
     energy = jnp.sum(misfit * valid / scale, axis=1)
-    total = lax.psum(energy, "pix")
+    total = jnp.sum(lax.all_gather(energy, "pix"), axis=0)
     return (chosen, total[None, :])
 
 

time: 70.1 us -> 72.3 us (1.031)
  local copies, waits for them, and re-layouts: 15 us -> 16.7 us
    psum x1 -> x0, blocking collectives: 6.17 us -> none  [per_device(): total = lax.psum(energy, 'pix')]
    unnamed x0 -> x1, blocking collectives: none -> 5.63 us
    unnamed x4 -> x7, local copies, waits for them, and re-layouts: 1.1 us -> 2.63 us
where the time goes in v1:
time: 72.3 us; the launch traced here: 72.1 us
  blocking collectives  38.9 us (54%)
  local copies, waits for them, and re-layouts  16.7 us (23%)
  other arithmetic  7.5 us (10%)
  matrix products  7.34 us (10%)
  between operations  1.42 us (2%)
    all_gather x1, blocking collectives, per_device(): piece = lax.all_gather(bundles, 'blk', axis=0, tiled=True)  33.2 us
    unnamed x1, blocking collectives  5.63 us
    dot_general x8, matrix products, sweep(): jnp.einsum('nsm,nmk->nsk', state, gram, precision=lax.Precision.HIGHEST)  5.45 us
    scatter x1, local copies, waits for them, and re-layouts, per_device(): flat = jnp.zeros((count * cap, bands), jnp.bfloat16).at[slots].set(pixels)  5.28 us
    another operation x3, other arithmetic  4.61 us
    scatter x1, local copies, waits for them, and re-layouts, per_device(): jnp.zeros((count * cap,), jnp.float32).at[slots].set(1.0)  4.32 us
    gather x1, local copies, waits for them, and re-layouts, per_device(): chosen = state.reshape(count * cap, width)[slots]  2.81 us
    unnamed x7, local copies, waits for them, and re-layouts  2.63 us

profile of v1, /device:TPU:0, one launch (start us, length us, event | category | flops | bytes accessed | tf_op | source)
XLA Modules:
  0.0 72.1 jit_solution(12030111681565185113)
XLA Ops:
  0.6 0.0 copy-start
  0.6 1.3 %dynamic-slice = u32[1]{0:T(128)} dynamic-slice(u32[32]{0:T(128)} %constant.40, u32[]{:T(128)S(6)} %add.40), dynamic_slice_sizes={1} | dynamic-slice | bytes 12
  2.6 0.7 fusion.11
  3.3 4.5 %reduce-window.6 = s32[16,8,128]{2,1,0:T(8,128)S(1)} reduce-window(s32[16,8,128]{2,1,0:T(8,128)S(1)} %fusion.11, s32[]{:T(128)} %constant.5.clone.1), window={size=1x1x128 pad=0_0x0_0x127_0}, to_apply=%region_2.3 | reduce-window | flops 2080768 | bytes 131076 | tf_op jit(solution)/shard_map/reduce-window
  7.8 0.1 slice.10
  7.9 0.1 copy.25
  8.0 0.1 copy.26
  8.1 0.1 broadcast_add_fusion
  8.2 0.7 fusion.10
  8.9 0.7 compare_select_fusion
  9.6 4.3 %scatter_custom_fusion.1 = f32[2048]{0:T(1024)S(1)} fusion(s32[1024]{0:T(1024)S(1)} %bitcast.46, f32[1024]{0:T(1024)S(1)} %broadcast.53, f32[]{:T(128)} %constant.17.clone.1), kind=kCustom, calls=%fused_computation.28 | custom fusion | bytes 8196 | tf_op jit(solution)/shard_map/scatter | solution.py:52
  14.0 33.2 %all_gather.9 = bf16[16,224,64]{1,2,0:T(8,128)(2,1)S(1)} all-gather(bf16[2,224,64]{1,2,0:T(8,128)(2,1)} %param.6), channel_id=1, replica_groups=mesh['blk'=8,'pix'=4] {'blk'}, dimensions={0}, use_global_device_ids=true | all-gather | bytes 516096 | tf_op jit(solution)/shard_map/all_gather | solution.py:53
  47.2 0.0 copy-done
  47.2 0.2 copy.27
  47.4 5.3 %scatter_custom_fusion = bf16[2048,224]{1,0:T(8,128)(2,1)S(1)} fusion(s32[1024]{0:T(1024)S(1)} %bitcast.48, bf16[1024,224]{1,0:T(8,128)(2,1)S(1)} %copy.27, bf16[]{:T(256)} %constant.21.clone.1), kind=kCustom, calls=%fused_computation.14 | custom fusion | bytes 917506 | tf_op jit(solution)/shard_map/scatter | solution.py:50
  52.7 0.5 convolution_add_fusion
  53.2 0.6 copy.29
  53.8 0.3 abs_reduce_fusion
  54.1 0.1 reduce_max.9
  54.3 6.0 %while.11 = (s32[]{:T(128)}, f32[16,128,64]{1,2,0:T(8,128)S(1)}, f32[16]{0:T(128)S(1)}, f32[16,64,64]{1,2,0:T(8,128)S(1)}, f32[16,128,64]{1,2,0:T(8,128)S(1)}, /*index=5*/s32[]{:T(128)}, s32[]{:T(128)}) while((s32[]{:T(128)}, f32[16,128,64]{1,2,0:T(8,128)S(1)}, f32[16]{0:T(128)S(1)}, f32[16,64,64]{1,2,0:T(8,128)S(1)}, ...), condition=%wide.region_7.8_spmd.clone, body=%wide.region_6.7_spmd.clone.sunk | while | flops 101449728 | bytes 2883735 | solution.py:35
  54.3 0.7 fusion.28
  55.1 0.7 fusion.28
  55.8 0.7 fusion.28
  56.6 0.7 fusion.28
  57.3 0.7 fusion.28
  58.1 0.7 fusion.28
  58.8 0.7 fusion.28
  59.6 0.7 fusion.28
  60.3 1.1 %multiply_reduce_fusion = f32[16,128]{1,0:T(8,128)S(1)} fusion(bf16[16,128,224]{1,2,0:T(8,128)(2,1)S(1)} %copy.29, f32[16,128,64]{1,2,0:T(8,128)S(1)} %get-tuple-element.29, bf16[16,224,64]{1,2,0:T(8,128)(2,1)S(1)} %all_gather.9), kind=kOutput, calls=%fused_computation.11 | convolution fusion | flops 354154496 | bytes 1908736 | tf_op jit(solution)/shard_map/nsm,nbm->nsb/dot_general | solution.py:36
  61.4 0.1 fusion.13
  61.5 0.2 dynamic-update-slice
  61.8 5.6 %all-reduce = f32[64]{0:T(128)S(1)} all-reduce(f32[64]{0:T(128)S(1)} %dynamic-update-slice), channel_id=2, replica_groups=mesh['blk'=8,'pix'=4] {'pix'}, use_global_device_ids=true, to_apply=%add | all-reduce | flops 64 | bytes 512
  67.4 0.1 reshape.67
  67.5 0.5 reduce_sum.49
  68.0 0.3 copy.30
  68.4 2.8 %gather_fusion = f32[1024,64]{1,0:T(8,128)S(1)} fusion(f32[2048,64]{1,0:T(8,128)S(1)} %bitcast.39, s32[1024]{0:T(1024)S(1)} %broadcast_clamp_fusion), kind=kCustom, calls=%fused_computation | custom fusion | bytes 528384 | tf_op jit(solution)/shard_map/gather | solution.py:56
  71.2 0.9 %copy.32 = f32[1024,64]{0,1:T(8,128)} copy(f32[1024,64]{1,0:T(8,128)S(1)} %gather_fusion) | data formatting | bytes 524288
  (16 shorter events, 0.3 us)
Async XLA Ops:
  0.6 46.6 %copy-start = (bf16[1024,224]{0,1:T(8,128)(2,1)S(1)}, bf16[1024,224]{0,1:T(8,128)(2,1)}, u32[]{:S(2)}) copy-start(bf16[1024,224]{0,1:T(8,128)(2,1)} %param.5) | copy-start | bytes 1376260
